TPU v7x, 256 devices: a whole 4x4x8 slice. The times are simulated.
256 devices in a mesh: row: 16 (over z, core), col: 16 (over x, y).
Axes of the slice: x: 4, y: 4, z: 8, core: 2. Of those that a mesh axis runs over, the one named last changes fastest.
Arguments:
- genotypes: int32 [4096, 16384], P(('row', 'col')), may hold values from 0 to 2, as said below
- snp_index: int32 [4096], P(('row', 'col')), may hold values from 0 to 16383, as said below
- freq_table: float32 [16384], replicated, as said below
- prior: float32 [16384, 16384], P('row', 'col'), as said below
- start_vectors: float32 [16384, 20], P('row'), may hold values from -6 to 6
Outputs:
- grm: float32 [16384, 16384], P('row', 'col')
- pcs: float32 [16384, 20], P('col')
- spectrum: float32 [3, 20], replicated
Inputs may be any that keep to these rules, and one draw needn't show every extreme that they name: `genotypes`: genotype dosages 0, 1 or 2. `snp_index`: strictly increasing; entry j lies in 4 * j to 4 * j + 3. `freq_table`: frequencies are multiples of 1/1024 between 52/1024 and 512/1024. `prior`: exactly symmetric; diagonal between 1 and 2, off-diagonal entries small.
All inputs are finite; a program needn't handle non-finite values.
Results may differ from a plain program's by a relative error of at most 0.0075.
Values may be sent and summed in bfloat16 or wider, within the bound.
No kernel may reach another device: no remote copies, remote signals or barrier semaphores. Data moves between devices by JAX's collectives and lax.ppermute only.
A program may use at most 128 MiB of HBM per device.

v0:
```python
import jax
import jax.numpy as jnp
from jax import lax
from jax.sharding import Mesh
from jax.sharding import PartitionSpec as P

S = 16384
ITERS = 3
COL = ("col_0", "col_1")
ROW_COL = ("row", "col_0", "col_1")


def total_of_pieces(array, axis):
    return lax.all_gather(array, axis).sum(0)


def copy_for_each(array, axis):
    length = lax.axis_size(axis)
    return lax.all_to_all(
        jnp.broadcast_to(array[None], (length, *array.shape)), axis, 0, 0, tiled=True
    )


def taken_together(array, axis):
    return copy_for_each(array, axis).sum(axis=0)


def in_one(arrays, axis):
    ravelled, at, outs = (jnp.concatenate([a.reshape(-1) for a in arrays]), 0, [])
    so_far = taken_together(ravelled, axis)
    for a in arrays:
        outs.append(so_far[at : at + a.size].reshape(a.shape))
        at += a.size
    return tuple(outs)


def one_axis_at_a_time(array, axes):
    for axis in axes:
        array = lax.psum(array, axis)
    return array


def standardize(genotypes, allele_freq):
    doubled = 2.0 * allele_freq
    spread = jnp.sqrt(doubled * (1.0 - allele_freq))
    return (genotypes.astype(jnp.float32) - doubled[:, None]) / spread[:, None]


def orthonormal(factor, image):
    return lax.linalg.triangular_solve(factor, image, left_side=False, lower=True, transpose_a=True)


def apply_tile(tile, vectors, transposed):
    if transposed:
        return lax.dot_general(tile, vectors, (((0,), (0,)), ((), ())))
    return jnp.dot(tile, vectors)


def local_gram(image):
    return jnp.dot(image.T, image)


def body(genotypes, snp_index, freq_table, prior, start_vectors):
    allele_freq = jnp.take(freq_table, snp_index)
    standard = standardize(genotypes, allele_freq).astype(jnp.bfloat16)
    row_count = lax.axis_size("row")
    col_count = lax.axis_size(COL)
    own_snps = genotypes.shape[0]
    total_snps = own_snps * row_count * col_count
    row_piece = lax.all_to_all(standard, "row", split_axis=1, concat_axis=0, tiled=True)
    col_piece = lax.all_to_all(standard, COL, split_axis=1, concat_axis=0, tiled=True)
    col_piece = col_piece.reshape(col_count, 1, own_snps, col_piece.shape[1])
    col_panel = lax.all_gather(col_piece, "row", axis=1, tiled=True)
    col_panel = col_panel.reshape(total_snps, col_panel.shape[3])
    window = lax.dot_general(
        lax.all_gather(row_piece, COL, axis=0, tiled=True),
        col_panel,
        (((0,), (0,)), ((), ())),
        preferred_element_type=jnp.float32,
    )
    grm = prior + window / total_snps
    scaled_start = start_vectors / jnp.sqrt(jnp.float32(S))
    diagonals = []
    image = total_of_pieces(apply_tile(grm, scaled_start, True), "row")
    for step in range(1, ITERS):
        if step % 2 == 1:
            product, gram = in_one((apply_tile(grm, image, False), local_gram(image)), COL)
        else:
            product, gram = (
                total_of_pieces(apply_tile(grm, image, True), "row"),
                total_of_pieces(local_gram(image), "row"),
            )
        factor = jnp.linalg.cholesky(gram)
        diagonals.append(jnp.diagonal(factor))
        image = orthonormal(factor, product)
    gram = one_axis_at_a_time(local_gram(image), COL)
    factor = jnp.linalg.cholesky(gram)
    diagonals.append(jnp.diagonal(factor))
    vectors = orthonormal(factor, image)
    pcs = vectors * jnp.sqrt(jnp.float32(S))
    spectrum = jnp.stack(diagonals, axis=0)
    return (grm, pcs, spectrum)


def solution(mesh):
    finer = Mesh(mesh.devices.reshape(mesh.shape["row"], 4, 4), ("row", "col_0", "col_1"))
    in_specs = (P(ROW_COL, None), P(ROW_COL), P(), P("row", COL), P("row", None))
    out_specs = (P("row", COL), P(COL, None), P())
    return jax.shard_map(body, mesh=finer, in_specs=in_specs, out_specs=out_specs, check_vma=False)
```

profile of v0, /device:TPU:32, one launch (start us, length us, event | category | flops | bytes accessed | tf_op | source)
XLA Modules:
  0.0 351.4 jit_solution(14662210511644327606)
XLA Ops:
  9.3 1.4 divide_convert_fusion
  10.8 18.3 %all_to_all.38 = bf16[16,16,1024]{2,0,1:T(8,128)(2,1)S(1)} all-to-all(bf16[16,16,1024]{2,0,1:T(8,128)(2,1)S(1)} %bitcast.82), channel_id=1, replica_groups=mesh['row'=16,'col_0'=4,'col_1'=4] {'col_0','col_1'}, dimensions={1} | all-to-all | bytes 1048576 | tf_op jit(solution)/shard_map/all_to_all | solution.py:71
  29.1 1.1 copy.44
  30.3 25.6 %all_to_all.39 = bf16[16,16,1024]{2,0,1:T(8,128)(2,1)} all-to-all(bf16[16,16,1024]{2,0,1:T(8,128)(2,1)S(1)} %bitcast.83), channel_id=1, replica_groups=mesh['row'=16,'col_0'=4,'col_1'=4] {'row'}, dimensions={1} | all-to-all | bytes 1048576 | tf_op jit(solution)/shard_map/all_to_all | solution.py:70
  55.9 37.5 %all-gather.12.cloned.1.call-done = bf16[16,256,1024]{2,0,1:T(8,128)(2,1)} async-done(((bf16[16,16,1024]{2,0,1:T(8,128)(2,1)}), bf16[16,256,1024]{2,0,1:T(8,128)(2,1)}) %all-gather.12.cloned.1.call-update) | async-done | bytes 8388624 | tf_op jit(solution)/shard_map/all_gather | solution.py:73
  93.5 11.3 %copy.45 = bf16[16,256,1024]{2,1,0:T(8,128)(2,1)} copy(bf16[16,256,1024]{2,0,1:T(8,128)(2,1)} %all-gather.12.cloned.1.call-done) | data formatting | bytes 16777216 | tf_op jit(solution)/shard_map/all_gather | solution.py:73
  104.8 63.9 %all-gather.10.cloned.1.call-done = bf16[4096,1024]{1,0:T(8,128)(2,1)} async-done(((bf16[256,1024]{1,0:T(8,128)(2,1)}), bf16[4096,1024]{1,0:T(8,128)(2,1)}) %all-gather.10.cloned.1.call-update) | async-done | bytes 8388624 | tf_op jit(solution)/shard_map/all_gather | solution.py:76
  168.6 14.4 %multiply_add_fusion = f32[1024,1024]{1,0:T(8,128)S(1)} fusion(f32[1024,1024]{1,0:T(8,128)} %param.11, bf16[4096,1024]{1,0:T(8,128)(2,1)} %all-gather.10.cloned.1.call-done, bf16[4096,1024]{1,0:T(8,128)(2,1)} %bitcast.79), kind=kOutput, calls=%fused_computation.4 | convolution fusion | flops 8592031744 | bytes 25165824 | tf_op jit(solution)/shard_map/dot_general | solution.py:75
  183.0 2.0 copy-done.1
  186.3 38.1 %all-gather.14.cloned.1.call-done = f32[16384,20]{0,1:T(8,128)} async-done(((f32[1024,20]{0,1:T(8,128)}), f32[16384,20]{0,1:T(8,128)}) %all-gather.14.cloned.1.call-update) | async-done | bytes 1310736 | tf_op jit(solution)/shard_map/all_gather | solution.py:14
  224.4 2.5 copy.58
  229.2 27.1 %all_to_all.40 = f32[16,1,20880]{2,1,0:T(1,128)S(1)} all-to-all(f32[16,1,20880]{2,1,0:T(1,128)S(1)} %broadcast_in_dim.22), channel_id=1, replica_groups=mesh['row'=16,'col_0'=4,'col_1'=4] {'col_0','col_1'}, dimensions={0} | all-to-all | bytes 2672640 | tf_op jit(solution)/shard_map/all_to_all | solution.py:19
  257.3 1.8 cholesky.59
  260.5 1.5 custom-call.13
  263.2 3.2 fusion.27
  266.6 15.7 %all-gather.4 = f32[16,20,20]{2,1,0:T(8,128)S(1)} all-gather(f32[1,20,20]{2,1,0:T(8,128)S(1)} %convolution_bitcast_fusion.3), channel_id=4, replica_groups=mesh['row'=16,'col_0'=4,'col_1'=4] {'row'}, dimensions={0}, use_global_device_ids=true | all-gather | bytes 27200 | tf_op jit(solution)/shard_map/all_gather | solution.py:14
  282.4 1.8 cholesky.70
  285.6 1.5 custom-call.14
  288.7 12.4 %all-gather.16.cloned.1.call-done = f32[16384,20]{0,1:T(8,128)} async-done(((f32[1024,20]{0,1:T(8,128)}), f32[16384,20]{0,1:T(8,128)}) %all-gather.16.cloned.1.call-update) | async-done | bytes 1310736 | tf_op jit(solution)/shard_map/all_gather | solution.py:14
  301.1 2.3 copy.59
  304.1 16.8 %psum.14 = f32[20,20]{0,1:T(8,128)S(1)} all-reduce(f32[20,20]{0,1:T(8,128)S(1)} %fusion.28), channel_id=1, replica_groups=mesh['row'=16,'col_0'=4,'col_1'=4] {'col_0'}, use_global_device_ids=true, to_apply=%region_6.9 | all-reduce | flops 400 | bytes 3200 | tf_op jit(solution)/shard_map/psum | solution.py:39
  320.9 16.8 %psum.15 = f32[20,20]{0,1:T(8,128)S(1)} all-reduce(f32[20,20]{0,1:T(8,128)S(1)} %psum.14), channel_id=1, replica_groups=mesh['row'=16,'col_0'=4,'col_1'=4] {'col_1'}, use_global_device_ids=true, to_apply=%region_7.10 | all-reduce | flops 400 | bytes 3200 | tf_op jit(solution)/shard_map/psum | solution.py:39
  337.8 1.8 cholesky.81
  341.8 1.5 custom-call.15
  (61 shorter events, 17.0 us)
Async XLA Ops:
  7.2 0.8 copy-start
  7.2 86.3 %all-gather.12.cloned.1.call-start = ((), (), s32[]{:S(2)}) async-start(), calls=%async_computation.4 | async-start | bytes 8912896 | tf_op jit(solution)/shard_map/all_gather | solution.py:73
  30.2 138.4 %all-gather.10.cloned.1.call-start = ((), (), s32[]{:S(2)}) async-start(), calls=%async_computation.3 | async-start | bytes 8912896 | tf_op jit(solution)/shard_map/all_gather | solution.py:76
  55.9 168.6 %all-gather.14.cloned.1.call-start = ((), (), s32[]{:S(2)}) async-start(), calls=%async_computation.5 | async-start | bytes 1671168 | tf_op jit(solution)/shard_map/all_gather | solution.py:14
  168.6 16.4 %copy-start.3 = (f32[1024,20]{0,1:T(8,128)S(1)}, f32[1024,20]{0,1:T(8,128)}, u32[]{:S(2)}) copy-start(f32[1024,20]{0,1:T(8,128)} %param.12) | copy-start | bytes 245764
  183.0 2.0 copy-start.1
  186.1 115.0 %all-gather.16.cloned.1.call-start = ((), (), s32[]{:S(2)}) async-start(), calls=%async_computation.6 | async-start | bytes 1671168 | tf_op jit(solution)/shard_map/all_gather | solution.py:14
  224.4 2.7 copy-start.2
Sparse Core Ops, SparseCore 0:
  30.4 63.0 all-gather.11
  95.9 72.6 all-gather.9
  186.2 38.1 all-gather.13
  266.6 34.5 all-gather.15
where the time goes:
time: 352 us; the launch traced here: 351 us
  waiting for transfers between devices  152 us (43%)
  blocking collectives  120 us (34%)
  local copies, waits for them, and re-layouts  24.6 us (7%)
  matrix products  21.5 us (6%)
  other arithmetic  18.7 us (5%)
  between operations  13.9 us (4%)
    all_gather x1, waiting for transfers between devices, body(): lax.all_gather(row_piece, COL, axis=0, tiled=True)  63.9 us
    all_gather x2, waiting for transfers between devices, total_of_pieces(): return lax.all_gather(array, axis).sum(0)  50.5 us
    all_gather x1, waiting for transfers between devices, body(): col_panel = lax.all_gather(col_piece, 'row', axis=1, tiled=True)  37.5 us
    psum x2, blocking collectives, one_axis_at_a_time(): array = lax.psum(array, axis)  33.6 us
    all_to_all x1, blocking collectives, copy_for_each(): lax.all_to_all(jnp.broadcast_to(array[None], (length, *array.shape)), axi...  27.1 us
    all_to_all x1, blocking collectives, body(): lax.all_to_all(standard, 'row', split_axis=1, concat_axis=0, tiled=True)  25.6 us
    all_to_all x1, blocking collectives, body(): lax.all_to_all(standard, COL, split_axis=1, concat_axis=0, tiled=True)  18.3 us
    all_gather x1, blocking collectives, total_of_pieces(): return lax.all_gather(array, axis).sum(0)  15.7 us
  transfers between devices with their start and end apart: 4, of which 4 were waited for; matrix products, arithmetic and copies ran while one was open for 5% of the time, Pallas kernels for 0%

commit v1 on v0

--- a/solution.py
+++ b/solution.py
@@ -8,6 +8,27 @@
 ITERS = 3
 COL = ("col_0", "col_1")
 ROW_COL = ("row", "col_0", "col_1")
+
+
+def collect(shard, axis, dim):
+    devices, index, width = (lax.axis_size(axis), lax.axis_index(axis), shard.shape[dim])
+    upward = [(i, (i + 1) % devices) for i in range(devices)]
+    backward = [(i, (i - 1) % devices) for i in range(devices)]
+    result = jnp.zeros((*shard.shape[:dim], devices * width, *shard.shape[dim + 1 :]), shard.dtype)
+    result = lax.dynamic_update_slice_in_dim(result, shard, index * width, axis=dim)
+    from_left = from_right = shard
+    half = devices // 2
+    for step in range(1, half + 1):
+        from_left = lax.ppermute(from_left, axis, upward)
+        result = lax.dynamic_update_slice_in_dim(
+            result, from_left, (index - step) % devices * width, axis=dim
+        )
+        if step < devices - half:
+            from_right = lax.ppermute(from_right, axis, backward)
+            result = lax.dynamic_update_slice_in_dim(
+                result, from_right, (index + step) % devices * width, axis=dim
+            )
+    return result
 
 
 def total_of_pieces(array, axis):
@@ -70,7 +91,7 @@
     row_piece = lax.all_to_all(standard, "row", split_axis=1, concat_axis=0, tiled=True)
     col_piece = lax.all_to_all(standard, COL, split_axis=1, concat_axis=0, tiled=True)
     col_piece = col_piece.reshape(col_count, 1, own_snps, col_piece.shape[1])
-    col_panel = lax.all_gather(col_piece, "row", axis=1, tiled=True)
+    col_panel = collect(col_piece, "row", 1)
     col_panel = col_panel.reshape(total_snps, col_panel.shape[3])
     window = lax.dot_general(
         lax.all_gather(row_piece, COL, axis=0, tiled=True),

time: 352 us -> 317 us (0.901)
  waiting for transfers between devices: 152 us -> 91.5 us
  starting transfers between devices: 0.35 us -> 17.5 us
  local copies, waits for them, and re-layouts: 24.6 us -> 32.7 us
    all_gather x1, waiting for transfers between devices: 63.9 us -> 0.01 us  [body(): lax.all_gather(row_piece, COL, axis=0, tiled=True)]
    ppermute x0 -> x15, waiting for transfers between devices: none -> 39.9 us  [the longest x8 37.4 us: collect(): from_left = lax.ppermute(from_left, axis, upward)]
    all_gather x1 -> x0, waiting for transfers between devices: 37.5 us -> none  [body(): col_panel = lax.all_gather(col_piece, 'row', axis=1, tiled=True)]
    ppermute x0 -> x15, starting transfers between devices: none -> 17.4 us  [the longest x7 17.4 us: collect(): from_right = lax.ppermute(from_right, axis, backward)]
    dynamic_update_slice x0 -> x16, local copies, waits for them, and re-layouts: none -> 16.3 us  [the longest x8 8.71 us: collect(): lax.dynamic_update_slice_in_dim(result, from_left, (index - step) % devic...]
    all_gather x1 -> x0, local copies, waits for them, and re-layouts: 11.3 us -> none  [body(): col_panel = lax.all_gather(col_piece, 'row', axis=1, tiled=True)]
    broadcast_in_dim x0 -> x1, local copies, waits for them, and re-layouts: none -> 4.28 us  [collect(): jnp.zeros((*shard.shape[:dim], devices * width, *shard.shape[dim + 1:]),...]
  transfers between devices with their start and end apart: 4 -> 18, of which waited for: 4 -> 12; matrix products, arithmetic and copies ran while one was open for 5% -> 9% of each run, Pallas kernels for 0% -> 0%
where the time goes in v1:
time: 317 us; the launch traced here: 316 us
  blocking collectives  118 us (37%)
  waiting for transfers between devices  91.5 us (29%)
  local copies, waits for them, and re-layouts  32.7 us (10%)
  matrix products  23.7 us (7%)
  other arithmetic  18.7 us (6%)
  starting transfers between devices  17.5 us (6%)
  between operations  13.9 us (4%)
    all_gather x2, waiting for transfers between devices, total_of_pieces(): return lax.all_gather(array, axis).sum(0)  51.5 us
    ppermute x8, waiting for transfers between devices, collect(): from_left = lax.ppermute(from_left, axis, upward)  37.4 us
    psum x2, blocking collectives, one_axis_at_a_time(): array = lax.psum(array, axis)  33.5 us
    all_to_all x1, blocking collectives, copy_for_each(): lax.all_to_all(jnp.broadcast_to(array[None], (length, *array.shape)), axi...  27.1 us
    all_to_all x1, blocking collectives, body(): lax.all_to_all(standard, 'row', split_axis=1, concat_axis=0, tiled=True)  22.7 us
    all_to_all x1, blocking collectives, body(): lax.all_to_all(standard, COL, split_axis=1, concat_axis=0, tiled=True)  19 us
    ppermute x7, starting transfers between devices, collect(): from_right = lax.ppermute(from_right, axis, backward)  17.4 us
    all_gather x1, blocking collectives, total_of_pieces(): return lax.all_gather(array, axis).sum(0)  15.7 us
  transfers between devices with their start and end apart: 18, of which 12 were waited for; matrix products, arithmetic and copies ran while one was open for 9% of the time, Pallas kernels for 0%

profile of v1, /device:TPU:32, one launch (start us, length us, event | category | flops | bytes accessed | tf_op | source)
XLA Modules:
  0.0 316.0 jit_solution(5876782824358746015)
XLA Ops:
  10.8 22.7 %all_to_all.38 = bf16[16,16,1024]{2,0,1:T(8,128)(2,1)} all-to-all(bf16[16,16,1024]{2,0,1:T(8,128)(2,1)S(1)} %bitcast.84), channel_id=1, replica_groups=mesh['row'=16,'col_0'=4,'col_1'=4] {'row'}, dimensions={1} | all-to-all | bytes 1048576 | tf_op jit(solution)/shard_map/all_to_all | solution.py:91
  33.6 19.0 %all_to_all.39 = bf16[16,16,1024]{2,0,1:T(8,128)(2,1)S(1)} all-to-all(bf16[16,16,1024]{2,0,1:T(8,128)(2,1)S(1)} %bitcast.85), channel_id=1, replica_groups=mesh['row'=16,'col_0'=4,'col_1'=4] {'col_0','col_1'}, dimensions={1} | all-to-all | bytes 1048576 | tf_op jit(solution)/shard_map/all_to_all | solution.py:92
  52.5 3.0 collective-permute-start.1
  55.5 6.9 %collective-permute-done = bf16[16,1,16,1024]{3,2,1,0:T(8,128)(2,1)S(1)} collective-permute-done((bf16[16,1,16,1024]{3,2,1,0:T(8,128)(2,1)S(1)}, bf16[16,1,16,1024]{3,2,1,0:T(8,128)(2,1)S(1)}, u32[]{:S(2)}, u32[]{:S(2)}) %collective-permute-start) | collective-permute-done | bytes 524320 | tf_op jit(solution)/shard_map/ppermute | solution.py:22
  64.2 6.9 %collective-permute-done.2 = bf16[16,1,16,1024]{3,2,1,0:T(8,128)(2,1)S(1)} collective-permute-done((bf16[16,1,16,1024]{3,2,1,0:T(8,128)(2,1)S(1)}, bf16[16,1,16,1024]{3,2,1,0:T(8,128)(2,1)S(1)}, u32[]{:S(2)}, u32[]{:S(2)}) %collective-permute-start.2) | collective-permute-done | bytes 524320 | tf_op jit(solution)/shard_map/ppermute | solution.py:22
  73.1 6.6 %collective-permute-done.4 = bf16[16,1,16,1024]{3,2,1,0:T(8,128)(2,1)S(1)} collective-permute-done((bf16[16,1,16,1024]{3,2,1,0:T(8,128)(2,1)S(1)}, bf16[16,1,16,1024]{3,2,1,0:T(8,128)(2,1)S(1)}, u32[]{:S(2)}, u32[]{:S(2)}) %collective-permute-start.4) | collective-permute-done | bytes 524320 | tf_op jit(solution)/shard_map/ppermute | solution.py:22
  79.8 2.3 collective-permute-start.7
  82.1 6.3 %collective-permute-done.6 = bf16[16,1,16,1024]{3,2,1,0:T(8,128)(2,1)} collective-permute-done((bf16[16,1,16,1024]{3,2,1,0:T(8,128)(2,1)S(1)}, bf16[16,1,16,1024]{3,2,1,0:T(8,128)(2,1)}, u32[]{:S(2)}, u32[]{:S(2)}) %collective-permute-start.6) | collective-permute-done | bytes 524320 | tf_op jit(solution)/shard_map/ppermute | solution.py:22
  88.8 2.3 collective-permute-start.9
  91.1 6.2 %collective-permute-done.8 = bf16[16,1,16,1024]{3,2,1,0:T(8,128)(2,1)} collective-permute-done((bf16[16,1,16,1024]{3,2,1,0:T(8,128)(2,1)}, bf16[16,1,16,1024]{3,2,1,0:T(8,128)(2,1)}, u32[]{:S(2)}, u32[]{:S(2)}) %collective-permute-start.8) | collective-permute-done | bytes 524320 | tf_op jit(solution)/shard_map/ppermute | solution.py:22
  97.3 4.3 %broadcast_in_dim.25 = bf16[16,16,16,1024]{3,2,1,0:T(8,128)(2,1)} broadcast(bf16[]{:T(256)} %constant.150.clone.1), dimensions={} | broadcast | bytes 8388610 | tf_op jit(solution)/shard_map/broadcast_in_dim | solution.py:17
  113.3 4.2 %collective-permute-start.13 = (bf16[16,1,16,1024]{3,2,1,0:T(8,128)(2,1)S(1)}, bf16[16,1,16,1024]{3,2,1,0:T(8,128)(2,1)S(1)}, u32[]{:S(2)}, u32[]{:S(2)}) collective-permute-start(bf16[16,1,16,1024]{3,2,1,0:T(8,128)(2,1)S(1)} %collective-permute-done.11), channel_id=1, source_target_pairs={{0,240},{16,0},{32,16},{48,32},{64,48},{80,64},{96,80},{112,96},{1... | collective-permute-start | bytes 1572872 | tf_op jit(solution)/shard_map/ppermute | solution.py:27
  125.0 4.6 %collective-permute-done.14 = bf16[16,1,16,1024]{3,2,1,0:T(8,128)(2,1)S(1)} collective-permute-done((bf16[16,1,16,1024]{3,2,1,0:T(8,128)(2,1)S(1)}, bf16[16,1,16,1024]{3,2,1,0:T(8,128)(2,1)S(1)}, u32[]{:S(2)}, u32[]{:S(2)}) %collective-permute-start.14) | collective-permute-done | bytes 524320 | tf_op jit(solution)/shard_map/ppermute | solution.py:22
  130.5 14.4 %multiply_add_fusion = f32[1024,1024]{1,0:T(8,128)S(1)} fusion(f32[1024,1024]{1,0:T(8,128)} %param.11, bf16[4096,1024]{1,0:T(8,128)(2,1)} %all-gather.8.cloned.1.call-done, bf16[4096,1024]{1,0:T(8,128)(2,1)} %bitcast.5), kind=kOutput, calls=%fused_computation.4 | convolution fusion | flops 8592031744 | bytes 25165824 | tf_op jit(solution)/shard_map/dot_general | solution.py:96
  148.0 39.0 %all-gather.10.cloned.1.call-done = f32[16384,20]{0,1:T(8,128)} async-done(((f32[1024,20]{0,1:T(8,128)}), f32[16384,20]{0,1:T(8,128)}) %all-gather.10.cloned.1.call-update) | async-done | bytes 1310736 | tf_op jit(solution)/shard_map/all_gather | solution.py:35
  187.1 2.3 copy.83
  189.6 2.9 fusion.25
  193.9 27.1 %all_to_all.40 = f32[16,1,20880]{2,1,0:T(1,128)S(1)} all-to-all(f32[16,1,20880]{2,1,0:T(1,128)S(1)} %broadcast_in_dim.26), channel_id=1, replica_groups=mesh['row'=16,'col_0'=4,'col_1'=4] {'col_0','col_1'}, dimensions={0} | all-to-all | bytes 2672640 | tf_op jit(solution)/shard_map/all_to_all | solution.py:40
  227.9 3.2 %fusion.27 = f32[1024,20]{0,1:T(8,128)} fusion(f32[1024,1024]{1,0:T(8,128)} %copy-done.1, bf16[1024,20]{0,1:T(8,128)(2,1)S(1)} %convolution_bitcast_fusion.2), kind=kOutput, calls=%fused_computation.71 | convolution fusion | flops 41943040 | bytes 4317184 | tf_op jit(solution)/shard_map/dot_general | solution.py:76
  231.3 15.7 %all-gather.3 = f32[16,20,20]{2,1,0:T(8,128)S(1)} all-gather(f32[1,20,20]{2,1,0:T(8,128)S(1)} %convolution_bitcast_fusion.3), channel_id=3, replica_groups=mesh['row'=16,'col_0'=4,'col_1'=4] {'row'}, dimensions={0}, use_global_device_ids=true | all-gather | bytes 27200 | tf_op jit(solution)/shard_map/all_gather | solution.py:35
  253.4 12.5 %all-gather.12.cloned.1.call-done = f32[16384,20]{0,1:T(8,128)} async-done(((f32[1024,20]{0,1:T(8,128)}), f32[16384,20]{0,1:T(8,128)}) %all-gather.12.cloned.1.call-update) | async-done | bytes 1310736 | tf_op jit(solution)/shard_map/all_gather | solution.py:35
  265.9 2.3 copy.84
  268.9 16.7 %psum.14 = f32[20,20]{0,1:T(8,128)S(1)} all-reduce(f32[20,20]{0,1:T(8,128)S(1)} %fusion.28), channel_id=1, replica_groups=mesh['row'=16,'col_0'=4,'col_1'=4] {'col_0'}, use_global_device_ids=true, to_apply=%region_6.9 | all-reduce | flops 400 | bytes 3200 | tf_op jit(solution)/shard_map/psum | solution.py:60
  285.6 16.8 %psum.15 = f32[20,20]{0,1:T(8,128)S(1)} all-reduce(f32[20,20]{0,1:T(8,128)S(1)} %psum.14), channel_id=1, replica_groups=mesh['row'=16,'col_0'=4,'col_1'=4] {'col_1'}, use_global_device_ids=true, to_apply=%region_7.10 | all-reduce | flops 400 | bytes 3200 | tf_op jit(solution)/shard_map/psum | solution.py:60
  (105 shorter events, 53.9 us)
Async XLA Ops:
  7.2 0.8 copy-start
  7.2 123.3 %all-gather.8.cloned.1.call-start = ((), (), s32[]{:S(2)}) async-start(), calls=%async_computation.3 | async-start | bytes 8912896 | tf_op jit(solution)/shard_map/all_gather | solution.py:97
  33.5 153.5 %all-gather.10.cloned.1.call-start = ((), (), s32[]{:S(2)}) async-start(), calls=%async_computation.4 | async-start | bytes 1671168 | tf_op jit(solution)/shard_map/all_gather | solution.py:35
  52.5 9.9 %collective-permute-start = (bf16[16,1,16,1024]{3,2,1,0:T(8,128)(2,1)S(1)}, bf16[16,1,16,1024]{3,2,1,0:T(8,128)(2,1)S(1)}, u32[]{:S(2)}, u32[]{:S(2)}) collective-permute-start(bf16[16,1,16,1024]{3,2,1,0:T(8,128)(2,1)S(1)} %bitcast.87), channel_id=1, source_target_pairs={{0,16},{16,32},{32,48},{48,64},{64,80},{80,96},{96,112},{112,128},... | collective-permute-start | bytes 1572872 | tf_op jit(solution)/shard_map/ppermute | solution.py:22
  52.5 9.9 %collective-permute-start.1 = (bf16[16,1,16,1024]{3,2,1,0:T(8,128)(2,1)S(1)}, bf16[16,1,16,1024]{3,2,1,0:T(8,128)(2,1)S(1)}, u32[]{:S(2)}, u32[]{:S(2)}) collective-permute-start(bf16[16,1,16,1024]{3,2,1,0:T(8,128)(2,1)S(1)} %bitcast.88), channel_id=1, source_target_pairs={{0,240},{16,0},{32,16},{48,32},{64,48},{80,64},{96,80},{112,96},{1... | collective-permute-start | bytes 1572872 | tf_op jit(solution)/shard_map/ppermute | solution.py:27
  62.4 8.6 %collective-permute-start.2 = (bf16[16,1,16,1024]{3,2,1,0:T(8,128)(2,1)S(1)}, bf16[16,1,16,1024]{3,2,1,0:T(8,128)(2,1)S(1)}, u32[]{:S(2)}, u32[]{:S(2)}) collective-permute-start(bf16[16,1,16,1024]{3,2,1,0:T(8,128)(2,1)S(1)} %collective-permute-done), channel_id=1, source_target_pairs={{0,16},{16,32},{32,48},{48,64},{64,80},{80,96},{96,112},{112,128},... | collective-permute-start | bytes 1572872 | tf_op jit(solution)/shard_map/ppermute | solution.py:22
  62.4 8.6 %collective-permute-start.3 = (bf16[16,1,16,1024]{3,2,1,0:T(8,128)(2,1)S(1)}, bf16[16,1,16,1024]{3,2,1,0:T(8,128)(2,1)S(1)}, u32[]{:S(2)}, u32[]{:S(2)}) collective-permute-start(bf16[16,1,16,1024]{3,2,1,0:T(8,128)(2,1)S(1)} %collective-permute-done.1), channel_id=1, source_target_pairs={{0,240},{16,0},{32,16},{48,32},{64,48},{80,64},{96,80},{112,96},{1... | collective-permute-start | bytes 1572872 | tf_op jit(solution)/shard_map/ppermute | solution.py:27
  71.0 17.3 %copy-start.2 = (bf16[16,1,16,1024]{3,2,1,0:T(8,128)(2,1)}, bf16[16,1,16,1024]{3,2,1,0:T(8,128)(2,1)S(1)}, u32[]{:S(2)}) copy-start(bf16[16,1,16,1024]{3,2,1,0:T(8,128)(2,1)S(1)} %collective-permute-done.2) | copy-start | bytes 1572868
  71.0 8.6 %collective-permute-start.4 = (bf16[16,1,16,1024]{3,2,1,0:T(8,128)(2,1)S(1)}, bf16[16,1,16,1024]{3,2,1,0:T(8,128)(2,1)S(1)}, u32[]{:S(2)}, u32[]{:S(2)}) collective-permute-start(bf16[16,1,16,1024]{3,2,1,0:T(8,128)(2,1)S(1)} %collective-permute-done.2), channel_id=1, source_target_pairs={{0,16},{16,32},{32,48},{48,64},{64,80},{80,96},{96,112},{112,128},... | collective-permute-start | bytes 1572872 | tf_op jit(solution)/shard_map/ppermute | solution.py:22
  71.0 8.7 %collective-permute-start.5 = (bf16[16,1,16,1024]{3,2,1,0:T(8,128)(2,1)S(1)}, bf16[16,1,16,1024]{3,2,1,0:T(8,128)(2,1)S(1)}, u32[]{:S(2)}, u32[]{:S(2)}) collective-permute-start(bf16[16,1,16,1024]{3,2,1,0:T(8,128)(2,1)S(1)} %collective-permute-done.3), channel_id=1, source_target_pairs={{0,240},{16,0},{32,16},{48,32},{64,48},{80,64},{96,80},{112,96},{1... | collective-permute-start | bytes 1572872 | tf_op jit(solution)/shard_map/ppermute | solution.py:27
  79.6 8.7 %collective-permute-start.6 = (bf16[16,1,16,1024]{3,2,1,0:T(8,128)(2,1)S(1)}, bf16[16,1,16,1024]{3,2,1,0:T(8,128)(2,1)}, u32[]{:S(2)}, u32[]{:S(2)}) collective-permute-start(bf16[16,1,16,1024]{3,2,1,0:T(8,128)(2,1)S(1)} %collective-permute-done.4), channel_id=1, source_target_pairs={{0,16},{16,32},{32,48},{48,64},{64,80},{80,96},{96,112},{112,128},... | collective-permute-start | bytes 1572872 | tf_op jit(solution)/shard_map/ppermute | solution.py:22
  79.8 9.0 %collective-permute-start.7 = (bf16[16,1,16,1024]{3,2,1,0:T(8,128)(2,1)S(1)}, bf16[16,1,16,1024]{3,2,1,0:T(8,128)(2,1)}, u32[]{:S(2)}, u32[]{:S(2)}) collective-permute-start(bf16[16,1,16,1024]{3,2,1,0:T(8,128)(2,1)S(1)} %collective-permute-done.5), channel_id=1, source_target_pairs={{0,240},{16,0},{32,16},{48,32},{64,48},{80,64},{96,80},{112,96},{1... | collective-permute-start | bytes 1572872 | tf_op jit(solution)/shard_map/ppermute | solution.py:27
  88.3 8.9 %collective-permute-start.8 = (bf16[16,1,16,1024]{3,2,1,0:T(8,128)(2,1)}, bf16[16,1,16,1024]{3,2,1,0:T(8,128)(2,1)}, u32[]{:S(2)}, u32[]{:S(2)}) collective-permute-start(bf16[16,1,16,1024]{3,2,1,0:T(8,128)(2,1)} %collective-permute-done.6), channel_id=1, source_target_pairs={{0,16},{16,32},{32,48},{48,64},{64,80},{80,96},{96,112},{112,128},... | collective-permute-start | bytes 1572872 | tf_op jit(solution)/shard_map/ppermute | solution.py:22
  88.3 15.7 %copy-start.3 = (bf16[16,1,16,1024]{3,2,1,0:T(8,128)(2,1)S(1)}, bf16[16,1,16,1024]{3,2,1,0:T(8,128)(2,1)}, u32[]{:S(2)}) copy-start(bf16[16,1,16,1024]{3,2,1,0:T(8,128)(2,1)} %copy-done.2) | copy-start | bytes 1572868
  88.8 16.1 %collective-permute-start.9 = (bf16[16,1,16,1024]{3,2,1,0:T(8,128)(2,1)}, bf16[16,1,16,1024]{3,2,1,0:T(8,128)(2,1)S(1)}, u32[]{:S(2)}, u32[]{:S(2)}) collective-permute-start(bf16[16,1,16,1024]{3,2,1,0:T(8,128)(2,1)} %collective-permute-done.7), channel_id=1, source_target_pairs={{0,240},{16,0},{32,16},{48,32},{64,48},{80,64},{96,80},{112,96},{1... | collective-permute-start | bytes 1572872 | tf_op jit(solution)/shard_map/ppermute | solution.py:27
  97.3 10.2 %collective-permute-start.10 = (bf16[16,1,16,1024]{3,2,1,0:T(8,128)(2,1)}, bf16[16,1,16,1024]{3,2,1,0:T(8,128)(2,1)S(1)}, u32[]{:S(2)}, u32[]{:S(2)}) collective-permute-start(bf16[16,1,16,1024]{3,2,1,0:T(8,128)(2,1)} %collective-permute-done.8), channel_id=1, source_target_pairs={{0,16},{16,32},{32,48},{48,64},{64,80},{80,96},{96,112},{112,128},... | collective-permute-start | bytes 1572872 | tf_op jit(solution)/shard_map/ppermute | solution.py:22
  104.8 8.5 %collective-permute-start.11 = (bf16[16,1,16,1024]{3,2,1,0:T(8,128)(2,1)S(1)}, bf16[16,1,16,1024]{3,2,1,0:T(8,128)(2,1)S(1)}, u32[]{:S(2)}, u32[]{:S(2)}) collective-permute-start(bf16[16,1,16,1024]{3,2,1,0:T(8,128)(2,1)S(1)} %collective-permute-done.9), channel_id=1, source_target_pairs={{0,240},{16,0},{32,16},{48,32},{64,48},{80,64},{96,80},{112,96},{1... | collective-permute-start | bytes 1572872 | tf_op jit(solution)/shard_map/ppermute | solution.py:27
  107.4 12.0 %collective-permute-start.12 = (bf16[16,1,16,1024]{3,2,1,0:T(8,128)(2,1)S(1)}, bf16[16,1,16,1024]{3,2,1,0:T(8,128)(2,1)S(1)}, u32[]{:S(2)}, u32[]{:S(2)}) collective-permute-start(bf16[16,1,16,1024]{3,2,1,0:T(8,128)(2,1)S(1)} %collective-permute-done.10), channel_id=1, source_target_pairs={{0,16},{16,32},{32,48},{48,64},{64,80},{80,96},{96,112},{112,128},... | collective-permute-start | bytes 1572872 | tf_op jit(solution)/shard_map/ppermute | solution.py:22
  113.3 10.9 %collective-permute-start.13 = (bf16[16,1,16,1024]{3,2,1,0:T(8,128)(2,1)S(1)}, bf16[16,1,16,1024]{3,2,1,0:T(8,128)(2,1)S(1)}, u32[]{:S(2)}, u32[]{:S(2)}) collective-permute-start(bf16[16,1,16,1024]{3,2,1,0:T(8,128)(2,1)S(1)} %collective-permute-done.11), channel_id=1, source_target_pairs={{0,240},{16,0},{32,16},{48,32},{64,48},{80,64},{96,80},{112,96},{1... | collective-permute-start | bytes 1572872 | tf_op jit(solution)/shard_map/ppermute | solution.py:27
  119.4 10.3 %collective-permute-start.14 = (bf16[16,1,16,1024]{3,2,1,0:T(8,128)(2,1)S(1)}, bf16[16,1,16,1024]{3,2,1,0:T(8,128)(2,1)S(1)}, u32[]{:S(2)}, u32[]{:S(2)}) collective-permute-start(bf16[16,1,16,1024]{3,2,1,0:T(8,128)(2,1)S(1)} %collective-permute-done.12), channel_id=1, source_target_pairs={{0,16},{16,32},{32,48},{48,64},{64,80},{80,96},{96,112},{112,128},... | collective-permute-start | bytes 1572872 | tf_op jit(solution)/shard_map/ppermute | solution.py:22
  130.5 16.4 %copy-start.4 = (f32[1024,20]{0,1:T(8,128)S(1)}, f32[1024,20]{0,1:T(8,128)}, u32[]{:S(2)}) copy-start(f32[1024,20]{0,1:T(8,128)} %param.12) | copy-start | bytes 245764
  144.9 2.0 copy-start.1
  148.0 117.9 %all-gather.12.cloned.1.call-start = ((), (), s32[]{:S(2)}) async-start(), calls=%async_computation.5 | async-start | bytes 1671168 | tf_op jit(solution)/shard_map/all_gather | solution.py:35
Sparse Core Ops, SparseCore 0:
  33.7 75.8 all-gather.7
  148.1 38.9 all-gather.9
  231.2 34.5 all-gather.11
